TPU v7x, 32 devices: a whole 2x2x4 slice. The times are simulated.
32 devices in a mesh: kv: 16 (over z, y, core), batch: 2 (over x).
Axes of the slice: x: 2, y: 2, z: 4, core: 2. Of those that a mesh axis runs over, the one named last changes fastest.
Arguments:
- queries: bfloat16 [32, 4, 32, 128], P(('kv', 'batch')), may hold values from -200 to 200
- prefix_keys: bfloat16 [2048, 16, 128], P(('kv', 'batch')), may hold values from -12 to 12
- prefix_values: bfloat16 [2048, 16, 128], P(('kv', 'batch')), may hold values from -12 to 12
- suffix_keys: bfloat16 [32, 1024, 16, 128], P(('kv', 'batch')), may hold values from -14 to 14
- suffix_values: bfloat16 [32, 1024, 16, 128], P(('kv', 'batch')), may hold values from -12 to 12
- lengths: int32 [32], P(('kv', 'batch')), may hold values from 256 to 1024, as said below
Outputs:
- attended: bfloat16 [32, 4, 32, 128], P(('kv', 'batch'))
Inputs may be any that keep to these rules, and one draw needn't show every extreme that they name: `lengths`: each sequence's own cache holds its 4 new tokens in its last used slots; some sequence fills all 1024 slots.
All inputs are finite; a program needn't handle non-finite values.
Results may differ from a plain program's by a relative error of at most 0.0045.
Values may be sent and summed in bfloat16 or wider, within the bound.
A program may use at most 64 MiB of HBM per device.

v0:
```python
import jax
import jax.numpy as jnp
from jax import lax
from jax.sharding import PartitionSpec as P

QUERY_SCALE = 144


masked_score = -1e30


def body(queries, prefix_keys, prefix_values, suffix_keys, suffix_values, lengths):
    scaling = QUERY_SCALE ** (-0.5)
    slab_keys, slab_values = (
        lax.all_gather(prefix_keys, "batch", axis=0, tiled=True),
        lax.all_gather(prefix_values, "batch", axis=0, tiled=True),
    )
    group_rows = lax.all_gather(queries, "kv", axis=0, tiled=True)
    count, new_tokens, heads, depth = group_rows.shape
    kv_heads = slab_keys.shape[1]
    queries_per_group = heads // kv_heads
    shaped = group_rows.reshape(count, new_tokens, kv_heads, queries_per_group, depth)
    scores = (
        jnp.einsum("bjgrd,pgd->bjgrp", shaped, slab_keys, preferred_element_type=jnp.float32)
        * scaling
    )
    top_prompt = jnp.max(scores, -1)
    weights = jnp.exp(scores - top_prompt[..., None])
    sum_prompt = jnp.sum(weights, -1)
    out_prompt = jnp.einsum(
        "bjgrp,pgd->bjgrd",
        weights.astype(jnp.bfloat16),
        slab_values,
        preferred_element_type=jnp.float32,
    )
    partial_value = (
        out_prompt.reshape(count, new_tokens, heads, depth),
        top_prompt.reshape(count, new_tokens, heads),
        sum_prompt.reshape(count, new_tokens, heads),
    )
    own_count = queries.shape[0]
    received = (
        lax.all_to_all(partial_value[0], "kv", split_axis=0, concat_axis=0, tiled=True),
        lax.all_to_all(partial_value[1], "kv", split_axis=0, concat_axis=0, tiled=True),
        lax.all_to_all(partial_value[2], "kv", split_axis=0, concat_axis=0, tiled=True),
    )
    sources = count // own_count
    outs_all = received[0].reshape(sources, own_count, new_tokens, heads, depth)
    tops_all = received[1].reshape(sources, own_count, new_tokens, heads)
    sums_all = received[2].reshape(sources, own_count, new_tokens, heads)
    top_p = jnp.max(tops_all, 0)
    factors = jnp.exp(tops_all - top_p[None])
    out_p = jnp.sum(outs_all * factors[..., None], 0)
    sum_p = jnp.sum(sums_all * factors, 0)
    own_shaped = queries.reshape(own_count, new_tokens, kv_heads, queries_per_group, depth)
    suffix_scores = (
        jnp.einsum("sjgrd,stgd->sjgrt", own_shaped, suffix_keys, preferred_element_type=jnp.float32)
        * scaling
    )
    slots = suffix_keys.shape[1]
    limits = lengths[:, None] - new_tokens + 1 + jnp.arange(new_tokens, dtype=jnp.int32)[None, :]
    visible = jnp.arange(slots, dtype=jnp.int32)[None, None, :] < limits[:, :, None]
    suffix_scores = jnp.where(visible[:, :, None, None, :], suffix_scores, masked_score)
    top_own = jnp.max(suffix_scores, -1)
    own_weights = jnp.exp(suffix_scores - top_own[..., None])
    sum_own = jnp.sum(own_weights, -1)
    out_own = jnp.einsum(
        "sjgrt,stgd->sjgrd",
        own_weights.astype(jnp.bfloat16),
        suffix_values,
        preferred_element_type=jnp.float32,
    )
    out_own = out_own.reshape(own_count, new_tokens, heads, depth)
    top_own = top_own.reshape(own_count, new_tokens, heads)
    sum_own = sum_own.reshape(own_count, new_tokens, heads)
    larger = jnp.maximum(top_p, top_own)
    factor_prompt = jnp.exp(top_p - larger)
    factor_own = jnp.exp(top_own - larger)
    numerator = out_p * factor_prompt[..., None] + out_own * factor_own[..., None]
    total = sum_p * factor_prompt + sum_own * factor_own
    return (numerator / total[..., None]).astype(jnp.bfloat16)


def solution(mesh):
    return jax.shard_map(
        body,
        mesh=mesh,
        in_specs=(
            P(("kv", "batch"), None, None, None),
            P(("kv", "batch"), None, None),
            P(("kv", "batch"), None, None),
            P(("kv", "batch"), None, None, None),
            P(("kv", "batch"), None, None, None),
            P(("kv", "batch")),
        ),
        out_specs=P(("kv", "batch"), None, None, None),
        check_vma=False,
    )
```

profile of v0, /device:TPU:1, one launch (start us, length us, event | category | flops | bytes accessed | tf_op | source)
XLA Modules:
  0.0 90.5 jit_solution(3657781256617135742)
XLA Ops:
  0.0 0.0 copy-start
  0.0 1.1 %copy.72 = bf16[64,16,128]{2,0,1:T(8,128)(2,1)S(1)} copy(bf16[64,16,128]{2,1,0:T(8,128)(2,1)} %param.7) | data formatting | bytes 524288 | tf_op args[1]
  1.1 8.7 %all_gather.9 = bf16[128,16,128]{2,0,1:T(8,128)(2,1)S(1)} all-gather(bf16[64,16,128]{2,0,1:T(8,128)(2,1)S(1)} %copy.72), channel_id=1, replica_groups=mesh['kv'=16,'batch'=2] {'batch'}, dimensions={0}, use_global_device_ids=true | all-gather | bytes 786432 | tf_op jit(solution)/shard_map/all_gather | solution.py:15
  9.8 24.8 %all_gather.10 = bf16[16,4,32,128]{3,2,1,0:T(8,128)(2,1)S(1)} all-gather(bf16[1,4,32,128]{3,2,1,0:T(8,128)(2,1)} %param.6), channel_id=1, replica_groups=mesh['kv'=16,'batch'=2] {'kv'}, dimensions={0}, use_global_device_ids=true | all-gather | bytes 557056 | tf_op jit(solution)/shard_map/all_gather | solution.py:18
  34.5 0.6 fusion.37
  35.2 0.8 fusion.17
  36.0 0.1 copy.89
  36.1 0.7 reshape.223
  36.8 3.4 %all-to-all-start.2 = ((f32[16,1,128]{2,1,0:T(1,128)}), f32[16,1,128]{2,1,0:T(1,128)S(1)}, u32[]{:S(2)}, u32[]{:S(2)}) async-start(f32[16,1,128]{2,1,0:T(1,128)} %reshape.223), calls=%async_computation.2 | async-start | bytes 16384 | tf_op jit(solution)/shard_map/all_to_all | solution.py:45
  40.2 0.0 copy-done
  40.2 0.1 copy.75
  40.3 8.3 %all_gather.11 = bf16[128,16,128]{2,0,1:T(8,128)(2,1)S(1)} all-gather(bf16[64,16,128]{2,0,1:T(8,128)(2,1)S(1)} %copy.75), channel_id=1, replica_groups=mesh['kv'=16,'batch'=2] {'batch'}, dimensions={0}, use_global_device_ids=true | all-gather | bytes 786432 | tf_op jit(solution)/shard_map/all_gather | solution.py:16
  48.6 0.1 copy.79
  48.7 0.7 reshape.221
  49.4 0.0 all-to-all-done.2
  49.4 6.8 %all-to-all-start.1 = ((f32[16,1,128]{2,1,0:T(1,128)}), f32[16,1,128]{2,1,0:T(1,128)S(1)}, u32[]{:S(2)}, u32[]{:S(2)}) async-start(f32[16,1,128]{2,1,0:T(1,128)} %reshape.221), calls=%async_computation.1 | async-start | bytes 16384 | tf_op jit(solution)/shard_map/all_to_all | solution.py:44
  56.2 0.0 copy-start.1
  56.2 0.5 convolution_bitcast_fusion
  56.7 0.1 copy.76
  56.8 1.3 %copy.77 = f32[16,4,32,128]{3,2,1,0:T(8,128)} copy(f32[16,4,32,128]{3,0,2,1:T(8,128)S(1)} %bitcast.54) | data formatting | bytes 2097152 | tf_op jit(solution)/shard_map/reshape | solution.py:37
  58.1 3.9 %all-to-all-done.1 = f32[16,1,128]{2,1,0:T(1,128)S(1)} async-done(((f32[16,1,128]{2,1,0:T(1,128)}), f32[16,1,128]{2,1,0:T(1,128)S(1)}, u32[]{:S(2)}, u32[]{:S(2)}) %all-to-all-start.1) | async-done | bytes 8224 | tf_op jit(solution)/shard_map/all_to_all | solution.py:44
  62.0 4.2 %all-to-all-start = ((f32[16,4,32,128]{3,2,1,0:T(8,128)}), f32[16,4,32,128]{3,2,1,0:T(8,128)S(1)}, u32[]{:S(2)}, u32[]{:S(2)}) async-start(f32[16,4,32,128]{3,2,1,0:T(8,128)} %copy.77), calls=%async_computation | async-start | bytes 2097152 | tf_op jit(solution)/shard_map/all_to_all | solution.py:43
  66.8 0.1 iota_compare_fusion
  66.9 0.0 copy-done.1
  66.9 4.7 %fusion.38 = (f32[4,16,2]{2,0,1:T(4,128)S(1)}, f32[1,4,16,2,1024]{4,3,1,2,0:T(2,128)S(1)}) fusion(bf16[4,16,2,128]{3,2,1,0:T(2,128)(2,1)S(1)} %bitcast.61, bf16[1024,16,128,1]{2,1,0,3:T(8,128)(2,1)} %bitcast.62, pred[4,1024]{1,0:T(4,128)(4,1)S(1)} %iota_compare_fusion), kind=kOutput, calls=%fused_computation.39 | convolution fusion | flops 33947520 | bytes 4755968 | tf_op jit(solution)/shard_map/sjgrd,stgd->sjgrt/dot_general | solution.py:57
  71.6 0.2 copy.83
  71.8 0.1 copy.84
  71.9 0.5 fusion.24
  72.4 0.2 copy.91
  72.6 0.1 copy.92
  72.7 4.7 %fusion.11 = f32[1,4,16,2,128]{4,3,1,2,0:T(2,128)S(1)} fusion(bf16[1024,16,128,1]{2,1,0,3:T(8,128)(2,1)} %bitcast.63, f32[1,4,16,2,1024]{4,3,1,2,0:T(2,128)S(1)} %get-tuple-element.13, f32[4,16,2]{2,0,1:T(4,128)S(1)} %get-tuple-element.12), kind=kOutput, calls=%fused_computation.9 | convolution fusion | flops 33816576 | bytes 4784640 | tf_op jit(solution)/shard_map/sjgrt,stgd->sjgrd/dot_general | solution.py:67
  77.4 0.5 broadcast.67
  77.9 0.7 reduce.9
  78.5 0.1 reshape.222
  78.6 0.7 reduce.8
  79.3 0.1 reshape.224
  79.5 9.9 %all-to-all-done = f32[16,4,32,128]{3,2,1,0:T(8,128)S(1)} async-done(((f32[16,4,32,128]{3,2,1,0:T(8,128)}), f32[16,4,32,128]{3,2,1,0:T(8,128)S(1)}, u32[]{:S(2)}, u32[]{:S(2)}) %all-to-all-start) | async-done | bytes 1048608 | tf_op jit(solution)/shard_map/all_to_all | solution.py:43
  89.4 0.3 multiply_reduce_fusion
  89.7 0.7 fusion.31
  (7 shorter events, 0.2 us)
Async XLA Ops:
  0.0 40.2 %copy-start = (bf16[64,16,128]{2,1,0:T(8,128)(2,1)S(1)}, bf16[64,16,128]{2,1,0:T(8,128)(2,1)}, u32[]{:S(2)}) copy-start(bf16[64,16,128]{2,1,0:T(8,128)(2,1)} %param.8) | copy-start | bytes 786436
  36.8 12.6 %all-to-all-start.2 = ((f32[16,1,128]{2,1,0:T(1,128)}), f32[16,1,128]{2,1,0:T(1,128)S(1)}, u32[]{:S(2)}, u32[]{:S(2)}) async-start(f32[16,1,128]{2,1,0:T(1,128)} %reshape.223), calls=%async_computation.2 | async-start | bytes 16384 | tf_op jit(solution)/shard_map/all_to_all | solution.py:45
  49.4 12.6 %all-to-all-start.1 = ((f32[16,1,128]{2,1,0:T(1,128)}), f32[16,1,128]{2,1,0:T(1,128)S(1)}, u32[]{:S(2)}, u32[]{:S(2)}) async-start(f32[16,1,128]{2,1,0:T(1,128)} %reshape.221), calls=%async_computation.1 | async-start | bytes 16384 | tf_op jit(solution)/shard_map/all_to_all | solution.py:44
  56.2 10.7 %copy-start.1 = (bf16[1,4,32,128]{3,2,1,0:T(8,128)(2,1)S(1)}, bf16[1,4,32,128]{3,2,1,0:T(8,128)(2,1)}, u32[]{:S(2)}) copy-start(bf16[1,4,32,128]{3,2,1,0:T(8,128)(2,1)} %param.6) | copy-start | bytes 98308
  62.0 27.4 %all-to-all-start = ((f32[16,4,32,128]{3,2,1,0:T(8,128)}), f32[16,4,32,128]{3,2,1,0:T(8,128)S(1)}, u32[]{:S(2)}, u32[]{:S(2)}) async-start(f32[16,4,32,128]{3,2,1,0:T(8,128)} %copy.77), calls=%async_computation | async-start | bytes 2097152 | tf_op jit(solution)/shard_map/all_to_all | solution.py:43
where the time goes:
time: 91.9 us; the launch traced here: 90.5 us
  blocking collectives  41.8 us (45%)
  starting transfers between devices  14.4 us (16%)
  waiting for transfers between devices  13.8 us (15%)
  matrix products  10.4 us (11%)
  local copies, waits for them, and re-layouts  5.4 us (6%)
  other arithmetic  3.88 us (4%)
    all_gather x1, blocking collectives, body(): group_rows = lax.all_gather(queries, 'kv', axis=0, tiled=True)  24.8 us
    all_to_all x1, waiting for transfers between devices, body(): lax.all_to_all(partial_value[0], 'kv', split_axis=0, concat_axis=0, tiled...  9.91 us
    all_gather x1, blocking collectives, body(): lax.all_gather(prefix_keys, 'batch', axis=0, tiled=True)  8.71 us
    all_gather x1, blocking collectives, body(): lax.all_gather(prefix_values, 'batch', axis=0, tiled=True)  8.3 us
    all_to_all x1, starting transfers between devices, body(): lax.all_to_all(partial_value[1], 'kv', split_axis=0, concat_axis=0, tiled...  6.8 us
    dot_general x1, matrix products, body(): jnp.einsum('sjgrd,stgd->sjgrt', own_shaped, suffix_keys, preferred_elemen...  4.68 us
    dot_general x1, matrix products, body(): jnp.einsum('sjgrt,stgd->sjgrd', own_weights.astype(jnp.bfloat16), suffix_...  4.66 us
    all_to_all x1, starting transfers between devices, body(): lax.all_to_all(partial_value[0], 'kv', split_axis=0, concat_axis=0, tiled...  4.16 us
  transfers between devices with their start and end apart: 3, of which 2 were waited for; matrix products, arithmetic and copies ran while one was open for 17% of the time, Pallas kernels for 0%

commit v1 on v0

v1 whole, which is shorter than its diff:
```python
import functools

import jax
import jax.numpy as jnp
from jax import lax
from jax.experimental import pallas as pl
from jax.experimental.pallas import tpu as pltpu
from jax.sharding import PartitionSpec as P

QUERY_SCALE = 144
MESH = pl.DeviceIdType.MESH
masked_score = -1e30
CHUNKS = 8


def dot_nt(a, b):
    return lax.dot_general(a, b, (((1,), (1,)), ((), ())), preferred_element_type=jnp.float32)


def kernel(
    sizes, length, q_hbm, kv_hbm, sk_hbm, sv_hbm, out_ref,
    qs, ks, vs, times, qa, qb, kva, kvb, oa, ob, la, lb, ra, rb, sa, sb,
    suffix_sem, local_sem, qa_send, qa_recv, qb_send, qb_recv,
    core_send, core_recv, xa_send, xa_recv, fa_send, fa_recv, yb_send, yb_recv,
    fb_send, fb_recv, oa_send, oa_recv, ob_send, ob_recv,
    la_send, la_recv, lb_send, lb_recv,
):
    deep, wide, new_tokens, rows, half, count_p, depth, kv_heads = sizes
    kv, x = lax.axis_index("kv"), lax.axis_index("batch")
    core, zy = kv % 2, kv // 2
    y, z = zy % 2, zy // 2
    na, nb = 2 * deep, deep * wide
    ia, ib = zy, z * wide + x
    scaling = QUERY_SCALE ** (-0.5)

    def device_a(i):
        return (i * 2 + core, x)

    def device_b(i):
        return ((i // wide * 2 + y) * 2 + core, i % wide)

    sibling = (kv + 1 - 2 * core, x)
    slot_a, slot_b = x * 2 + core, y * 2 + core

    locals_ = [
        pltpu.make_async_copy(q_hbm.at[0], qa.at[ia], local_sem.at[0]),
        pltpu.make_async_copy(q_hbm.at[1], qb.at[ib], local_sem.at[1]),
        pltpu.make_async_copy(kv_hbm.at[0], kva.at[slot_a], local_sem.at[2]),
        pltpu.make_async_copy(kv_hbm.at[1], kvb.at[slot_b], local_sem.at[3]),
        pltpu.make_async_copy(q_hbm, qs, local_sem.at[4]),
    ]
    for copy in locals_:
        copy.start()
    span = ks.shape[0] // CHUNKS
    loads = []
    for c in range(CHUNKS):
        part = pl.ds(c * span, span)
        loads.append((
            pltpu.make_async_copy(sk_hbm.at[part], ks.at[part], suffix_sem.at[0, c]),
            pltpu.make_async_copy(sv_hbm.at[part], vs.at[part], suffix_sem.at[1, c]),
        ))
        for copy in loads[-1]:
            copy.start()

    barrier = pltpu.get_barrier_semaphore()

    def peers(n, me, act):
        def step(k, carry):
            act(lax.rem(me + k, n))
            return carry

        lax.fori_loop(1, n, step, 0, unroll=n <= 16)

    def greet(device):
        pl.semaphore_signal(barrier, inc=1, device_id=device, device_id_type=MESH)

    greet(sibling)
    peers(na, ia, lambda i: greet(device_a(i)))
    peers(nb, ib, lambda i: greet(device_b(i)))
    pl.semaphore_wait(barrier, na + nb - 1)

    def remote(src, dst, send, recv, device):
        return pltpu.make_async_remote_copy(
            src_ref=src, dst_ref=dst, send_sem=send, recv_sem=recv,
            device_id=device, device_id_type=MESH,
        )

    for copy in locals_:
        copy.wait()
    q_a = lambda i, s: remote(qa.at[s], qa.at[s], qa_send.at[i], qa_recv.at[s], device_a(i))
    q_b = lambda i, s: remote(qb.at[s], qb.at[s], qb_send.at[i], qb_recv.at[s], device_b(i))
    peers(na, ia, lambda i: q_a(i, ia).start())
    peers(nb, ib, lambda i: q_b(i, ib).start())
    x_a = lambda i, s: remote(
        kva.at[s], kva.at[s], xa_send.at[i], xa_recv.at[s // 2], (kv, i))
    peers(wide, x, lambda i: x_a(i, slot_a).start())
    y_b = lambda s: remote(
        kvb.at[s], kvb.at[s], yb_send, yb_recv, ((z * 2 + 1 - y) * 2 + core, x))
    y_b(slot_b).start()
    c_a = lambda s: remote(kva.at[s], kva.at[s], core_send.at[0], core_recv.at[0], sibling)
    c_b = lambda s: remote(kvb.at[s], kvb.at[s], core_send.at[1], core_recv.at[1], sibling)
    c_a(slot_a).start()
    c_b(slot_b).start()

    total_rows = kv_heads * rows
    row = lax.broadcasted_iota(jnp.int32, (total_rows, span), 0)
    col = lax.broadcasted_iota(jnp.int32, (total_rows, span), 1)
    times[...] = jnp.where(row // rows == col % kv_heads, col // kv_heads, 2 ** 30)
    token = lax.broadcasted_iota(jnp.int32, (total_rows, 1), 0) % rows // (rows // new_tokens)
    limit = length[0] - new_tokens + 1 + token
    queries = jnp.concatenate([qs[0], qs[1]], axis=0)
    top = jnp.full((total_rows, 1), masked_score, jnp.float32)
    total = jnp.zeros((total_rows, 1), jnp.float32)
    acc = jnp.zeros((total_rows, depth), jnp.float32)
    for c in range(CHUNKS):
        for copy in loads[c]:
            copy.wait()
        part = pl.ds(c * span, span)
        scores = dot_nt(queries, ks[part]) * scaling
        scores = jnp.where(times[...] < limit - c * (span // kv_heads), scores, masked_score)
        higher = jnp.maximum(top, jnp.max(scores, -1, keepdims=True))
        weights = jnp.exp(scores - higher)
        fade = jnp.exp(top - higher)
        total = total * fade + jnp.sum(weights, -1, keepdims=True)
        acc = acc * fade + jnp.dot(
            weights.astype(jnp.bfloat16), vs[part], preferred_element_type=jnp.float32)
        top = higher
    own = acc / total
    own_level = top + jnp.log(total)

    f_a = lambda i, s: remote(kva.at[s], kva.at[s], fa_send.at[i], fa_recv.at[i], sibling)
    f_b = lambda s: remote(kvb.at[s], kvb.at[s], fb_send, fb_recv, sibling)

    def forward_a(i):
        x_a(i, i * 2 + core).wait_recv()
        f_a(i, i * 2 + core).start()

    peers(wide, x, forward_a)
    near = (1 - y) * 2 + core
    y_b(near).wait_recv()
    f_b(near).start()
    peers(na, ia, lambda i: q_a(i, i).wait_recv())
    peers(nb, ib, lambda i: q_b(i, i).wait_recv())
    c_a(slot_a).wait_recv()
    c_b(slot_b).wait_recv()

    def attend(n, qbuf, kvbuf, obuf, lbuf):
        blocks = kvbuf.shape[0]
        lane = lax.broadcasted_iota(jnp.int32, (n * rows, depth), 1)
        levels = jnp.zeros((n * rows, depth), jnp.float32)
        for g in range(half):
            part = pl.ds(g * rows, rows)
            q = qbuf[:, part, :].astype(jnp.float32).reshape(n * rows, depth).astype(jnp.bfloat16)
            k = kvbuf[:, 0, g].reshape(blocks * count_p, depth)
            v = kvbuf[:, 1, g].reshape(blocks * count_p, depth)
            s = dot_nt(q, k) * scaling
            m = jnp.max(s, -1, keepdims=True)
            w = jnp.exp(s - m)
            t = jnp.sum(w, -1, keepdims=True)
            o = jnp.dot(w.astype(jnp.bfloat16), v, preferred_element_type=jnp.float32) / t
            obuf[:, part, :] = o.reshape(n, rows, depth).astype(jnp.bfloat16)
            levels = jnp.where(lane == g, m + jnp.log(t), levels)
        lbuf[...] = levels.reshape(n, rows, depth)

    o_a = lambda i, s: remote(oa.at[i], ra.at[s], oa_send.at[i], oa_recv.at[s], device_a(i))
    o_b = lambda i, s: remote(ob.at[i], rb.at[s], ob_send.at[i], ob_recv.at[s], device_b(i))
    l_a = lambda i, s: remote(la.at[i], sa.at[s], la_send.at[i], la_recv.at[s], device_a(i))
    l_b = lambda i, s: remote(lb.at[i], sb.at[s], lb_send.at[i], lb_recv.at[s], device_b(i))

    f_b(near).wait_recv()
    attend(nb, qb, kvb, ob, lb)

    def send_b(i):
        o_b(i, ib).start()
        l_b(i, ib).start()

    peers(nb, ib, send_b)
    rb[ib] = ob[ib]
    sb[ib] = lb[ib]
    peers(wide, x, lambda i: f_a(i, i * 2 + core).wait_recv())
    attend(na, qa, kva, oa, la)

    def send_a(i):
        o_a(i, ia).start()
        l_a(i, ia).start()

    peers(na, ia, send_a)
    ra[ia] = oa[ia]
    sa[ia] = la[ia]

    def merge(n, first, rbuf, sbuf):
        lane = lax.broadcasted_iota(jnp.int32, (rows, depth), 1)
        mine = jnp.zeros((rows, depth), jnp.float32)
        for g in range(half):
            at = (first + g) * rows
            mine = jnp.where(lane == g, own_level[at : at + rows], mine)
        levels = sbuf[...]
        most = jnp.maximum(jnp.max(levels, 0), mine)
        factor, factor_mine = jnp.exp(levels - most), jnp.exp(mine - most)
        inverse = 1.0 / (jnp.sum(factor, 0) + factor_mine)
        factor, factor_mine = factor * inverse, factor_mine * inverse
        for g in range(half):
            at = (first + g) * rows
            result = own[at : at + rows] * factor_mine[:, g : g + 1]
            outs = rbuf[:, g * rows : (g + 1) * rows, :].astype(jnp.float32)
            result += jnp.sum(outs * factor[:, :, g : g + 1], 0)
            out_ref[at : at + rows] = result.astype(jnp.bfloat16)

    def arrive_b(i):
        o_b(i, i).wait_recv()
        l_b(i, i).wait_recv()

    def arrive_a(i):
        o_a(i, i).wait_recv()
        l_a(i, i).wait_recv()

    peers(nb, ib, arrive_b)
    merge(nb, half, rb, sb)
    peers(na, ia, arrive_a)
    merge(na, 0, ra, sa)

    def sent_a(i):
        q_a(i, ia).wait_send()
        o_a(i, ia).wait_send()
        l_a(i, ia).wait_send()

    def sent_b(i):
        q_b(i, ib).wait_send()
        o_b(i, ib).wait_send()
        l_b(i, ib).wait_send()

    def sent_x(i):
        x_a(i, slot_a).wait_send()
        f_a(i, i * 2 + core).wait_send()

    peers(na, ia, sent_a)
    peers(nb, ib, sent_b)
    peers(wide, x, sent_x)
    y_b(slot_b).wait_send()
    f_b(near).wait_send()
    c_a(slot_a).wait_send()
    c_b(slot_b).wait_send()


def body(deep, wide, queries, prefix_keys, prefix_values, suffix_keys, suffix_values, lengths):
    _, new_tokens, heads, depth = queries.shape
    count_p, kv_heads, _ = prefix_keys.shape
    slots = suffix_keys.shape[1]
    group = heads // kv_heads
    rows, half = new_tokens * group, kv_heads // 2
    q = queries.reshape(new_tokens, kv_heads, group, depth).transpose(1, 0, 2, 3)
    q = q.reshape(2, half * rows, depth)
    prompt = jnp.stack([prefix_keys, prefix_values])
    prompt = prompt.reshape(2, count_p, 2, half, depth).transpose(2, 0, 3, 1, 4)
    na, nb = 2 * deep, deep * wide
    dma = pltpu.SemaphoreType.DMA
    bf, f32 = jnp.bfloat16, jnp.float32
    flat = slots * kv_heads
    span = flat // CHUNKS
    out = pl.pallas_call(
        functools.partial(kernel, (deep, wide, new_tokens, rows, half, count_p, depth, kv_heads)),
        out_shape=jax.ShapeDtypeStruct((kv_heads * rows, depth), bf),
        in_specs=[pl.BlockSpec(memory_space=pltpu.SMEM)] + [pl.BlockSpec(memory_space=pl.ANY)] * 4,
        out_specs=pl.BlockSpec(memory_space=pltpu.VMEM),
        scratch_shapes=[
            pltpu.VMEM((2, half * rows, depth), bf),
            pltpu.VMEM((flat, depth), bf),
            pltpu.VMEM((flat, depth), bf),
            pltpu.VMEM((kv_heads * rows, span), jnp.int32),
            pltpu.VMEM((na, half * rows, depth), bf),
            pltpu.VMEM((nb, half * rows, depth), bf),
            pltpu.VMEM((2 * wide, 2, half, count_p, depth), bf),
            pltpu.VMEM((4, 2, half, count_p, depth), bf),
            pltpu.VMEM((na, half * rows, depth), bf),
            pltpu.VMEM((nb, half * rows, depth), bf),
            pltpu.VMEM((na, rows, depth), f32),
            pltpu.VMEM((nb, rows, depth), f32),
            pltpu.VMEM((na, half * rows, depth), bf),
            pltpu.VMEM((nb, half * rows, depth), bf),
            pltpu.VMEM((na, rows, depth), f32),
            pltpu.VMEM((nb, rows, depth), f32),
            dma((2, CHUNKS)), dma((5,)), dma((na,)), dma((na,)), dma((nb,)), dma((nb,)),
            dma((2,)), dma((2,)), dma((wide,)), dma((wide,)), dma((wide,)), dma((wide,)), dma, dma,
            dma, dma, dma((na,)), dma((na,)), dma((nb,)), dma((nb,)),
            dma((na,)), dma((na,)), dma((nb,)), dma((nb,)),
        ],
        compiler_params=pltpu.CompilerParams(
            collective_id=0, has_side_effects=True, vmem_limit_bytes=48 * 1024 * 1024
        ),
    )(lengths, q, prompt, suffix_keys.reshape(flat, depth), suffix_values.reshape(flat, depth))
    out = out.reshape(kv_heads, new_tokens, group, depth).transpose(1, 0, 2, 3)
    return out.reshape(1, new_tokens, heads, depth)


def solution(mesh):
    deep, wide = mesh.shape["kv"] // 4, mesh.shape["batch"]
    return jax.shard_map(
        functools.partial(body, deep, wide),
        mesh=mesh,
        in_specs=(
            P(("kv", "batch"), None, None, None),
            P(("kv", "batch"), None, None),
            P(("kv", "batch"), None, None),
            P(("kv", "batch"), None, None, None),
            P(("kv", "batch"), None, None, None),
            P(("kv", "batch")),
        ),
        out_specs=P(("kv", "batch"), None, None, None),
        check_vma=False,
    )
```

time: 91.9 us -> 33.6 us (0.37); the launches traced: 90.5 us -> 33.1 us
  blocking collectives: 41.8 us -> 0 us
  Pallas kernels: 0 us -> 26.7 us
  starting transfers between devices: 14.4 us -> 0 us
  waiting for transfers between devices: 13.8 us -> 0 us
  matrix products: 10.4 us -> 0 us
  other arithmetic: 3.88 us -> 0.05 us
    all_gather x3 -> x0, blocking collectives: 41.8 us -> none  [the longest x1 24.8 us: body(): group_rows = lax.all_gather(queries, 'kv', axis=0, tiled=True)]
    pallas_call x0 -> x1, Pallas kernels: none -> 26.7 us  [body(): pl.pallas_call(functools.partial(kernel, (deep, wide, new_tokens, rows, h...]
    all_to_all x3 -> x0, starting transfers between devices: 14.4 us -> none  [the longest x1 6.8 us: body(): lax.all_to_all(partial_value[1], 'kv', split_axis=0, concat_axis=0, tiled...]
    all_to_all x3 -> x0, waiting for transfers between devices: 13.8 us -> none  [the longest x1 9.91 us: body(): lax.all_to_all(partial_value[0], 'kv', split_axis=0, concat_axis=0, tiled...]
    dot_general x4 -> x0, matrix products: 10.5 us -> none  [the longest x1 4.68 us: body(): jnp.einsum('sjgrd,stgd->sjgrt', own_shaped, suffix_keys, preferred_elemen...]
    reduce_sum x4 -> x0, other arithmetic: 1.68 us -> none  [the longest x1 0.78 us: body(): sum_prompt = jnp.sum(weights, -1)]
    unnamed x10 -> x4, local copies, waits for them, and re-layouts: 2.69 us -> 4.22 us
    all_to_all x2 -> x0, other arithmetic: 1.34 us -> none  [the longest x1 0.67 us: body(): lax.all_to_all(partial_value[2], 'kv', split_axis=0, concat_axis=0, tiled...]
  transfers between devices with their start and end apart: 3 -> 0, of which waited for: 2 -> 0; matrix products, arithmetic and copies ran while one was open for 17% -> 0% of each run, Pallas kernels for 0% -> 0%
where the time goes in v1:
time: 33.6 us; the launch traced here: 33.1 us
  Pallas kernels  26.7 us (79%)
  local copies, waits for them, and re-layouts  5.65 us (17%)
  between operations  0.68 us (2%)
    pallas_call x1, Pallas kernels, body(): pl.pallas_call(functools.partial(kernel, (deep, wide, new_tokens, rows, h...  26.7 us
    unnamed x4, local copies, waits for them, and re-layouts  4.22 us
    reshape x1, local copies, waits for them, and re-layouts, body(): queries.reshape(new_tokens, kv_heads, group, depth).transpose(1, 0, 2, 3)  0.78 us

profile of v1, /device:TPU:1, one launch (start us, length us, event | category | flops | bytes accessed | tf_op | source)
XLA Modules:
  0.0 33.1 jit_solution(16886538857737597387)
XLA Ops:
  0.0 1.0 %copy.8 = bf16[64,16,128]{2,0,1:T(8,128)(2,1)S(1)} copy(bf16[64,16,128]{2,1,0:T(8,128)(2,1)} %param.7) | data formatting | bytes 524288 | tf_op args[1]
  1.0 1.0 %copy.9 = bf16[64,16,128]{2,0,1:T(8,128)(2,1)S(1)} copy(bf16[64,16,128]{2,1,0:T(8,128)(2,1)} %param.8) | data formatting | bytes 524288 | tf_op args[2]
  2.0 0.1 maximum_bitcast_fusion.kv_hbm
  2.1 0.8 %copy.7 = bf16[4,16,2,128]{3,2,0,1:T(2,128)(2,1)S(1)} copy(bf16[4,16,2,128]{3,2,1,0:T(2,128)(2,1)} %bitcast.20) | data formatting | bytes 65536 | tf_op jit(solution)/shard_map/reshape | solution.py:251
  3.5 0.0 copy-start
  3.6 2.2 %copy-done = bf16[1,1024,16,128]{3,2,1,0:T(8,128)(2,1)S(1)} copy-done((bf16[1,1024,16,128]{3,2,1,0:T(8,128)(2,1)S(1)}, bf16[1,1024,16,128]{3,2,1,0:T(8,128)(2,1)}, u32[]{:S(2)}) %copy-start) | copy-done | bytes 4194328
  5.7 26.7 %shard_map.64 = bf16[128,128]{1,0:T(8,128)(2,1)S(1)} custom-call(s32[1]{0:T(128)S(6)} %copy.11.length, bf16[2,64,128]{2,1,0:T(8,128)(2,1)S(1)} %bitcast.16, bf16[2,2,8,64,128]{4,3,2,1,0:T(8,128)(2,1)S(1)} %maximum_bitcast_fusion.kv_hbm, bf16[16384,128]{1,0:T(8,128)(2,1)S(1)} %bitcast.14, bf16[16384,128]{1,0:T(8,128)(2,1)} %bitcast.17), custom_call_target="tpu_custom_call" | custom-call | tf_op jit(solution)/shard_map/pallas_call | solution.py:260
  32.4 0.6 %copy.10 = bf16[4,16,2,128]{3,2,1,0:T(2,128)(2,1)} copy(bf16[4,16,2,128]{3,2,0,1:T(2,128)(2,1)S(1)} %bitcast.15) | data formatting | bytes 65536 | tf_op jit(solution)/shard_map/transpose | solution.py:291
Async XLA Ops:
  3.5 2.2 %copy-start = (bf16[1,1024,16,128]{3,2,1,0:T(8,128)(2,1)S(1)}, bf16[1,1024,16,128]{3,2,1,0:T(8,128)(2,1)}, u32[]{:S(2)}) copy-start(bf16[1,1024,16,128]{3,2,1,0:T(8,128)(2,1)} %param.9) | copy-start | bytes 12582916

commit v2 on v1

--- a/solution.py
+++ b/solution.py
@@ -18,8 +18,8 @@
 
 
 def kernel(
-    sizes, length, q_hbm, kv_hbm, sk_hbm, sv_hbm, out_ref,
-    qs, ks, vs, times, qa, qb, kva, kvb, oa, ob, la, lb, ra, rb, sa, sb,
+    sizes, length, q_hbm, pk_hbm, pv_hbm, sk_hbm, sv_hbm, out_ref,
+    qs, merged, pk, pv, ks, vs, times, qa, qb, kva, kvb, oa, ob, la, lb, ra, rb, sa, sb,
     suffix_sem, local_sem, qa_send, qa_recv, qb_send, qb_recv,
     core_send, core_recv, xa_send, xa_recv, fa_send, fa_recv, yb_send, yb_recv,
     fb_send, fb_recv, oa_send, oa_recv, ob_send, ob_recv,
@@ -43,11 +43,9 @@
     slot_a, slot_b = x * 2 + core, y * 2 + core
 
     locals_ = [
-        pltpu.make_async_copy(q_hbm.at[0], qa.at[ia], local_sem.at[0]),
-        pltpu.make_async_copy(q_hbm.at[1], qb.at[ib], local_sem.at[1]),
-        pltpu.make_async_copy(kv_hbm.at[0], kva.at[slot_a], local_sem.at[2]),
-        pltpu.make_async_copy(kv_hbm.at[1], kvb.at[slot_b], local_sem.at[3]),
-        pltpu.make_async_copy(q_hbm, qs, local_sem.at[4]),
+        pltpu.make_async_copy(q_hbm, qs, local_sem.at[0]),
+        pltpu.make_async_copy(pk_hbm, pk, local_sem.at[1]),
+        pltpu.make_async_copy(pv_hbm, pv, local_sem.at[2]),
     ]
     for copy in locals_:
         copy.start()
@@ -77,6 +75,22 @@
     greet(sibling)
     peers(na, ia, lambda i: greet(device_a(i)))
     peers(nb, ib, lambda i: greet(device_b(i)))
+    total_rows = kv_heads * rows
+    group = rows // new_tokens
+    ordered = lax.broadcasted_iota(jnp.int32, (total_rows, total_rows), 0)
+    natural = lax.broadcasted_iota(jnp.int32, (total_rows, total_rows), 1)
+    token_of = ordered % rows // group
+    source = token_of * (kv_heads * group) + ordered // rows * group + ordered % group
+    swap = jnp.where(source == natural, 1.0, 0.0).astype(jnp.bfloat16)
+    for copy in locals_:
+        copy.wait()
+    queries = jnp.dot(swap, qs[...], preferred_element_type=jnp.float32).astype(jnp.bfloat16)
+    qa[ia] = queries[: half * rows]
+    qb[ib] = queries[half * rows :]
+    for index, prompt in enumerate((pk, pv)):
+        block = jnp.swapaxes(prompt[...].astype(jnp.float32), 0, 1).astype(jnp.bfloat16)
+        kva[slot_a, index] = block[:half]
+        kvb[slot_b, index] = block[half:]
     pl.semaphore_wait(barrier, na + nb - 1)
 
     def remote(src, dst, send, recv, device):
@@ -85,8 +99,6 @@
             device_id=device, device_id_type=MESH,
         )
 
-    for copy in locals_:
-        copy.wait()
     q_a = lambda i, s: remote(qa.at[s], qa.at[s], qa_send.at[i], qa_recv.at[s], device_a(i))
     q_b = lambda i, s: remote(qb.at[s], qb.at[s], qb_send.at[i], qb_recv.at[s], device_b(i))
     peers(na, ia, lambda i: q_a(i, ia).start())
@@ -102,13 +114,11 @@
     c_a(slot_a).start()
     c_b(slot_b).start()
 
-    total_rows = kv_heads * rows
     row = lax.broadcasted_iota(jnp.int32, (total_rows, span), 0)
     col = lax.broadcasted_iota(jnp.int32, (total_rows, span), 1)
     times[...] = jnp.where(row // rows == col % kv_heads, col // kv_heads, 2 ** 30)
-    token = lax.broadcasted_iota(jnp.int32, (total_rows, 1), 0) % rows // (rows // new_tokens)
+    token = lax.broadcasted_iota(jnp.int32, (total_rows, 1), 0) % rows // group
     limit = length[0] - new_tokens + 1 + token
-    queries = jnp.concatenate([qs[0], qs[1]], axis=0)
     top = jnp.full((total_rows, 1), masked_score, jnp.float32)
     total = jnp.zeros((total_rows, 1), jnp.float32)
     acc = jnp.zeros((total_rows, depth), jnp.float32)
@@ -204,7 +214,7 @@
             result = own[at : at + rows] * factor_mine[:, g : g + 1]
             outs = rbuf[:, g * rows : (g + 1) * rows, :].astype(jnp.float32)
             result += jnp.sum(outs * factor[:, :, g : g + 1], 0)
-            out_ref[at : at + rows] = result.astype(jnp.bfloat16)
+            merged[at : at + rows] = result
 
     def arrive_b(i):
         o_b(i, i).wait_recv()
@@ -218,6 +228,9 @@
     merge(nb, half, rb, sb)
     peers(na, ia, arrive_a)
     merge(na, 0, ra, sa)
+    out_ref[...] = lax.dot_general(
+        swap, merged[...].astype(jnp.bfloat16), (((0,), (0,)), ((), ())),
+        preferred_element_type=jnp.float32).astype(jnp.bfloat16)
 
     def sent_a(i):
         q_a(i, ia).wait_send()
@@ -248,10 +261,7 @@
     slots = suffix_keys.shape[1]
     group = heads // kv_heads
     rows, half = new_tokens * group, kv_heads // 2
-    q = queries.reshape(new_tokens, kv_heads, group, depth).transpose(1, 0, 2, 3)
-    q = q.reshape(2, half * rows, depth)
-    prompt = jnp.stack([prefix_keys, prefix_values])
-    prompt = prompt.reshape(2, count_p, 2, half, depth).transpose(2, 0, 3, 1, 4)
+    q = queries.reshape(new_tokens * heads, depth)
     na, nb = 2 * deep, deep * wide
     dma = pltpu.SemaphoreType.DMA
     bf, f32 = jnp.bfloat16, jnp.float32
@@ -260,10 +270,13 @@
     out = pl.pallas_call(
         functools.partial(kernel, (deep, wide, new_tokens, rows, half, count_p, depth, kv_heads)),
         out_shape=jax.ShapeDtypeStruct((kv_heads * rows, depth), bf),
-        in_specs=[pl.BlockSpec(memory_space=pltpu.SMEM)] + [pl.BlockSpec(memory_space=pl.ANY)] * 4,
+        in_specs=[pl.BlockSpec(memory_space=pltpu.SMEM)] + [pl.BlockSpec(memory_space=pltpu.HBM)] * 5,
         out_specs=pl.BlockSpec(memory_space=pltpu.VMEM),
         scratch_shapes=[
-            pltpu.VMEM((2, half * rows, depth), bf),
+            pltpu.VMEM((kv_heads * rows, depth), bf),
+            pltpu.VMEM((kv_heads * rows, depth), f32),
+            pltpu.VMEM((count_p, kv_heads, depth), bf),
+            pltpu.VMEM((count_p, kv_heads, depth), bf),
             pltpu.VMEM((flat, depth), bf),
             pltpu.VMEM((flat, depth), bf),
             pltpu.VMEM((kv_heads * rows, span), jnp.int32),
@@ -279,16 +292,15 @@
             pltpu.VMEM((nb, half * rows, depth), bf),
             pltpu.VMEM((na, rows, depth), f32),
             pltpu.VMEM((nb, rows, depth), f32),
-            dma((2, CHUNKS)), dma((5,)), dma((na,)), dma((na,)), dma((nb,)), dma((nb,)),
+            dma((2, CHUNKS)), dma((3,)), dma((na,)), dma((na,)), dma((nb,)), dma((nb,)),
             dma((2,)), dma((2,)), dma((wide,)), dma((wide,)), dma((wide,)), dma((wide,)), dma, dma,
             dma, dma, dma((na,)), dma((na,)), dma((nb,)), dma((nb,)),
             dma((na,)), dma((na,)), dma((nb,)), dma((nb,)),
         ],
         compiler_params=pltpu.CompilerParams(
-            collective_id=0, has_side_effects=True, vmem_limit_bytes=48 * 1024 * 1024
+            collective_id=0, has_side_effects=True, vmem_limit_bytes=67043328
         ),
-    )(lengths, q, prompt, suffix_keys.reshape(flat, depth), suffix_values.reshape(flat, depth))
-    out = out.reshape(kv_heads, new_tokens, group, depth).transpose(1, 0, 2, 3)
+    )(lengths, q, prefix_keys, prefix_values, suffix_keys.reshape(flat, depth), suffix_values.reshape(flat, depth))
     return out.reshape(1, new_tokens, heads, depth)
 
 

time: 33.6 us -> 32 us (0.952); the launches traced: 33.1 us -> 31.9 us
  local copies, waits for them, and re-layouts: 5.65 us -> 1.38 us
  Pallas kernels: 26.7 us -> 29.8 us
    pallas_call x1, Pallas kernels: 26.7 us -> 29.8 us  [body(): pl.pallas_call(functools.partial(kernel, (deep, wide, new_tokens, rows, h...]
    unnamed x4 -> x1, local copies, waits for them, and re-layouts: 4.22 us -> 1.38 us
    reshape x1 -> x0, local copies, waits for them, and re-layouts: 0.78 us -> none  [body(): queries.reshape(new_tokens, kv_heads, group, depth).transpose(1, 0, 2, 3)]
    transpose x1 -> x0, local copies, waits for them, and re-layouts: 0.64 us -> none  [body(): out = out.reshape(kv_heads, new_tokens, group, depth).transpose(1, 0, 2, 3)]
where the time goes in v2:
time: 32 us; the launch traced here: 31.9 us
  Pallas kernels  29.8 us (93%)
  local copies, waits for them, and re-layouts  1.38 us (4%)
  between operations  0.66 us (2%)
    pallas_call x1, Pallas kernels, body(): pl.pallas_call(functools.partial(kernel, (deep, wide, new_tokens, rows, h...  29.8 us
    unnamed x1, local copies, waits for them, and re-layouts  1.38 us

profile of v2, /device:TPU:1, one launch (start us, length us, event | category | flops | bytes accessed | tf_op | source)
XLA Modules:
  0.0 31.9 jit_solution(1396532779664698014)
XLA Ops:
  0.7 29.8 %shard_map.64 = bf16[128,128]{1,0:T(8,128)(2,1)} custom-call(s32[1]{0:T(128)S(6)} %copy.8.length, bf16[128,128]{1,0:T(8,128)(2,1)} %bitcast.7, bf16[64,16,128]{2,1,0:T(8,128)(2,1)} %pk_hbm.1, bf16[64,16,128]{2,1,0:T(8,128)(2,1)} %pv_hbm.1, bf16[16384,128]{1,0:T(8,128)(2,1)} %bitcast.4, bf16[16384,128]{1,0:T(8,128)(2,1)} %bitcast.5), custom_call_target="tpu_custom_call" | custom-call | tf_op jit(solution)/shard_map/pallas_call | solution.py:270
  30.5 1.4 %copy.9 = bf16[1,4,32,128]{3,2,1,0:T(8,128)(2,1)} copy(bf16[1,4,32,128]{3,2,1,0:T(8,128)(2,1)} %bitcast.6) | data formatting | bytes 65536

commit v3 on v2

--- a/solution.py
+++ b/solution.py
@@ -49,16 +49,6 @@
     ]
     for copy in locals_:
         copy.start()
-    span = ks.shape[0] // CHUNKS
-    loads = []
-    for c in range(CHUNKS):
-        part = pl.ds(c * span, span)
-        loads.append((
-            pltpu.make_async_copy(sk_hbm.at[part], ks.at[part], suffix_sem.at[0, c]),
-            pltpu.make_async_copy(sv_hbm.at[part], vs.at[part], suffix_sem.at[1, c]),
-        ))
-        for copy in loads[-1]:
-            copy.start()
 
     barrier = pltpu.get_barrier_semaphore()
 
@@ -113,6 +103,17 @@
     c_b = lambda s: remote(kvb.at[s], kvb.at[s], core_send.at[1], core_recv.at[1], sibling)
     c_a(slot_a).start()
     c_b(slot_b).start()
+
+    span = ks.shape[0] // CHUNKS
+    loads = []
+    for c in range(CHUNKS):
+        part = pl.ds(c * span, span)
+        loads.append((
+            pltpu.make_async_copy(sk_hbm.at[part], ks.at[part], suffix_sem.at[0, c]),
+            pltpu.make_async_copy(sv_hbm.at[part], vs.at[part], suffix_sem.at[1, c]),
+        ))
+        for copy in loads[-1]:
+            copy.start()
 
     row = lax.broadcasted_iota(jnp.int32, (total_rows, span), 0)
     col = lax.broadcasted_iota(jnp.int32, (total_rows, span), 1)

time: 32 us -> 29.4 us (0.919)
  Pallas kernels: 29.8 us -> 27 us
    pallas_call x1, Pallas kernels: 29.8 us -> 27 us  [body(): pl.pallas_call(functools.partial(kernel, (deep, wide, new_tokens, rows, h...]
where the time goes in v3:
time: 29.4 us; the launch traced here: 29 us
  Pallas kernels  27 us (92%)
  local copies, waits for them, and re-layouts  1.38 us (5%)
  between operations  0.66 us (2%)
    pallas_call x1, Pallas kernels, body(): pl.pallas_call(functools.partial(kernel, (deep, wide, new_tokens, rows, h...  27 us
    unnamed x1, local copies, waits for them, and re-layouts  1.38 us

profile of v3, /device:TPU:1, one launch (start us, length us, event | category | flops | bytes accessed | tf_op | source)
XLA Modules:
  0.0 29.0 jit_solution(16072883765161796225)
XLA Ops:
  0.7 27.0 %shard_map.64 = bf16[128,128]{1,0:T(8,128)(2,1)} custom-call(s32[1]{0:T(128)S(6)} %copy.8.length, bf16[128,128]{1,0:T(8,128)(2,1)} %bitcast.7, bf16[64,16,128]{2,1,0:T(8,128)(2,1)} %pk_hbm.1, bf16[64,16,128]{2,1,0:T(8,128)(2,1)} %pv_hbm.1, bf16[16384,128]{1,0:T(8,128)(2,1)} %bitcast.4, bf16[16384,128]{1,0:T(8,128)(2,1)} %bitcast.5), custom_call_target="tpu_custom_call" | custom-call | tf_op jit(solution)/shard_map/pallas_call | solution.py:271
  27.6 1.4 %copy.9 = bf16[1,4,32,128]{3,2,1,0:T(8,128)(2,1)} copy(bf16[1,4,32,128]{3,2,1,0:T(8,128)(2,1)} %bitcast.6) | data formatting | bytes 65536
